TPU v7x, 256 devices: a whole 4x4x8 slice. The times are simulated.
256 devices in a mesh: mom: 64 (over z, y, core), idx: 4 (over x).
Axes of the slice: x: 4, y: 4, z: 8, core: 2. Of those that a mesh axis runs over, the one named last changes fastest.
Arguments:
- vertex: bfloat16 [3, 256, 512, 512], P(None, 'mom', None, 'idx'), may hold values from -0.25 to 0.25
- formfactors: bfloat16 [2048, 512], replicated, may hold values from -6 to 6
- propagator: float32 [256], replicated, may hold values from -4 to 4
- loop_mom: int32 [2048], replicated, may hold values from 0 to 255
- bond_disp: int32 [8, 2], replicated, may hold values from 0 to 15
- proj_channel: int32 [3, 8, 4], replicated, may hold values from 0 to 2
- proj_bond: int32 [3, 8, 4], replicated, may hold values from 0 to 7
- proj_phase: int32 [3, 8, 4], replicated, may hold values from 0 to 3
Outputs:
- flow: float32 [3, 256, 512, 512], P(None, 'mom', None, 'idx')
All inputs are finite; a program needn't handle non-finite values.
Results may differ from a plain program's by a relative error of at most 0.005.
Values may be sent and summed in bfloat16 or wider, within the bound.
No kernel may reach another device: no remote copies, remote signals or barrier semaphores. Data moves between devices by JAX's collectives and lax.ppermute only.
A program may use at most 128 MiB of HBM per device.

v0:
```python
import math

import jax
import jax.numpy as jnp
from jax import lax
from jax.experimental import pallas as pl
from jax.experimental.pallas import tpu as pltpu
from jax.sharding import Mesh
from jax.sharding import PartitionSpec as P

MSIDE = 16
NQ = 256
NI = 512
NL = 2048
NB = 8
SOURCES = 4
COLS = 128
GROUP = 64
OWNERS = 16
ROWS = NI // OWNERS
QUARTER = ROWS // 4
LCHUNK = 512


BF = jnp.bfloat16
F32 = jnp.float32


def cost(flops, nbytes):
    return pl.CostEstimate(flops=flops, bytes_accessed=nbytes, transcendentals=0)


def nt_dot(a, b):
    return lax.dot_general(a, b, (((1,), (1,)), ((), ())), preferred_element_type=F32)


def momentum_sum(former, latter, signed):
    coord_x = (former // MSIDE + signed * (latter // MSIDE)) % MSIDE
    coord_y = (former % MSIDE + signed * (latter % MSIDE)) % MSIDE
    return coord_x * MSIDE + coord_y


def lookup(values, indices):
    hits = indices[..., None] == jnp.arange(values.shape[0], dtype=jnp.int32)
    return jnp.sum(jnp.where(hits, values, 0.0), axis=-1)


def loop_weights(propagator, loop_mom, q):
    every = jnp.arange(NQ, dtype=jnp.int32)
    partners = jnp.stack(
        [momentum_sum(q, every, -1), momentum_sum(every, q, 1), momentum_sum(every, q, -1)]
    )
    table = jnp.concatenate([propagator[None, :], lookup(propagator, partners)], axis=0)
    hot = (every[:, None] == loop_mom[None, :]).astype(F32)
    found = jnp.einsum("nk,kl->nl", table, hot, precision=lax.Precision.HIGHEST)
    return found[0:1] * found[1:4] * (1.0 / math.sqrt(NL))


def phase_table(bond_disp, momenta):
    coord_x = momenta // MSIDE
    coord_y = momenta % MSIDE
    turns = (bond_disp[:, 0:1] * coord_x[None, :] + bond_disp[:, 1:2] * coord_y[None, :]) % MSIDE
    angles = turns.astype(F32) * (2.0 * math.pi / MSIDE)
    return jnp.concatenate([jnp.cos(angles), -jnp.sin(angles)], axis=0).astype(BF)


def spread(count, each):
    long = lax.broadcasted_iota(jnp.int32, (count * each, count), 0) // each
    short = lax.broadcasted_iota(jnp.int32, (count * each, count), 1)
    return (long == short).astype(BF)


def times_identity(matrix, each):
    rows, cols = matrix.shape
    wide = jnp.einsum("rc,kc->rk", matrix, spread(cols, each), preferred_element_type=F32)
    full = jnp.einsum(
        "mr,rk->mk", spread(rows, each), wide.astype(BF), preferred_element_type=F32
    )
    row_id = lax.broadcasted_iota(jnp.int32, full.shape, 0) % each
    col_id = lax.broadcasted_iota(jnp.int32, full.shape, 1) % each
    return jnp.where(row_id == col_id, full, 0.0)


def mixing_matrix(proj_channel, proj_bond, proj_phase):
    chan_hot = (proj_channel[..., None] == jnp.arange(3, dtype=jnp.int32)).astype(F32)
    bond_hot = (proj_bond[..., None] == jnp.arange(NB, dtype=jnp.int32)).astype(F32)
    direct = (proj_phase == 0).astype(F32) - (proj_phase == 2).astype(F32)
    crossed = (proj_phase == 3).astype(F32) - (proj_phase == 1).astype(F32)
    pair = (bond_hot[..., :, None] * chan_hot[..., None, :]).reshape(3, NB, SOURCES, 3 * NB)
    same = jnp.sum(pair * direct[..., None], axis=2)
    swapped = jnp.sum(pair * crossed[..., None], axis=2)
    same = jnp.swapaxes(same, 0, 1).reshape(3 * NB, 3 * NB)
    swapped = jnp.swapaxes(swapped, 0, 1).reshape(3 * NB, 3 * NB)
    upper = jnp.concatenate([same, swapped], axis=1)
    lower = jnp.concatenate([-swapped, same], axis=1)
    return (jnp.concatenate([upper, lower], axis=0) * (1.0 / MSIDE)).astype(BF)


def kernel_rows(panels, form, turned_form, weights, total):
    turned = jnp.concatenate([panel(c).T for panel in panels for c in range(3)], axis=0)
    count = 3 * len(panels)
    for step in range(NL // LCHUNK):
        low, high = step * LCHUNK, (step + 1) * LCHUNK
        terms = jnp.dot(turned, turned_form[:, low:high], preferred_element_type=F32)
        weighted = jnp.concatenate(
            [
                (
                    terms[k * COLS : (k + 1) * COLS] * weights[k % 3 : k % 3 + 1, low:high]
                ).astype(BF)
                for k in range(count)
            ],
            axis=0,
        )
        add = jnp.dot(weighted, form[low:high, :], preferred_element_type=F32)
        if step == 0:
            total[...] = add
        else:
            total[...] += add


def own_body(place, vertex, form, weights, out, turned_form, v0, total, sem):
    own = pltpu.make_async_copy(vertex.at[:, place[0]], v0, sem)
    own.start()
    for step in range(NL // LCHUNK):
        low, high = step * LCHUNK, (step + 1) * LCHUNK
        turned_form[:, low:high] = form[low:high, :].T
    own.wait()
    kernel_rows([lambda c: v0[c]], form, turned_form, weights, total)
    out[...] = total[...].astype(BF)


def panel_body(panel, form, turned_form, weights, out, total):
    kernel_rows([lambda c: panel[c]], form, turned_form, weights, total)
    out[...] = total[...].astype(BF)


def last_body(
    place, v0, v1, v2, v3, form, turned_form, weights, k0, k2, out, total, whole, k13, held, sems
):
    x = place[0]
    kernel_rows([lambda c: v1[c], lambda c: v3[c]], form, turned_form, weights, total)
    k13[...] = total[...].astype(BF)
    for c in range(3):
        for s in range(4):
            whole[c, lax.rem(x + 4 - s, 4)] = (v0, v1, v2, v3)[s][c]

    def copy(c):
        return pltpu.make_async_copy(held.at[c], out.at[:, :, c], sems.at[c])

    for c in range(3):
        row = c * COLS
        natural = jnp.concatenate([whole[c, n] for n in range(4)], axis=1)
        rows = jnp.concatenate(
            [
                k0[row : row + COLS],
                k13[row : row + COLS],
                k2[row : row + COLS],
                k13[3 * COLS + row : 3 * COLS + row + COLS],
            ],
            axis=0,
        )
        inc = nt_dot(natural, rows).astype(BF)
        for s in range(4):
            part = inc[:, s * COLS : (s + 1) * COLS].reshape(OWNERS, 1, ROWS, COLS)
            held[c, :, pl.ds(lax.rem(x + 4 - s, 4), 1)] = part
        if c > 0:
            copy(c - 1).start()
    copy(2).start()
    for c in range(3):
        copy(c).wait()


VM = pl.BlockSpec(memory_space=pltpu.VMEM)
SMALL = pltpu.CompilerParams(vmem_limit_bytes=24 << 20)
KERNEL_FLOPS = 2 * 2 * 3 * COLS * NL * NI


HB = pl.BlockSpec(memory_space=pltpu.HBM)
SM = pl.BlockSpec(memory_space=pltpu.SMEM)


def own_rows(place, vertex, form, weights):
    return pl.pallas_call(
        own_body,
        out_shape=[
            jax.ShapeDtypeStruct((3 * COLS, NI), BF),
            jax.ShapeDtypeStruct((NI, NL), BF),
            jax.ShapeDtypeStruct((3, NI, COLS), BF),
        ],
        in_specs=[SM, HB, VM, VM],
        out_specs=[VM] * 3,
        scratch_shapes=[pltpu.VMEM((3 * COLS, NI), F32), pltpu.SemaphoreType.DMA],
        cost_estimate=cost(KERNEL_FLOPS, 3 << 20),
        compiler_params=SMALL,
        name="own_rows",
    )(place, vertex, form, weights)


def panel_rows(panel, form, turned_form, weights):
    return pl.pallas_call(
        panel_body,
        out_shape=jax.ShapeDtypeStruct((3 * COLS, NI), BF),
        in_specs=[VM] * 4,
        out_specs=VM,
        scratch_shapes=[pltpu.VMEM((3 * COLS, NI), F32)],
        cost_estimate=cost(KERNEL_FLOPS, 3 << 20),
        compiler_params=SMALL,
        name="panel_rows",
    )(panel, form, turned_form, weights)


def last_rows(place, v0, v1, v2, v3, form, turned_form, weights, k0, k2):
    return pl.pallas_call(
        last_body,
        out_shape=jax.ShapeDtypeStruct((OWNERS, 4, 3, ROWS, COLS), BF),
        in_specs=[SM] + [VM] * 9,
        out_specs=HB,
        scratch_shapes=[
            pltpu.VMEM((6 * COLS, NI), F32),
            pltpu.VMEM((3, 4, NI, COLS), BF),
            pltpu.VMEM((6 * COLS, NI), BF),
            pltpu.VMEM((3, OWNERS, 4, ROWS, COLS), BF),
            pltpu.SemaphoreType.DMA((3,)),
        ],
        cost_estimate=cost(2 * KERNEL_FLOPS + 2 * 3 * NI * NI * NI, 8 << 20),
        compiler_params=SMALL,
        name="last_rows",
    )(place, v0, v1, v2, v3, form, turned_form, weights, k0, k2)


def forward_body(terms, matrix, out):
    for c in range(3):
        row = c * ROWS
        halves = [terms[:, row + h : row + h + 16, :].reshape(GROUP * 16, COLS) for h in (0, 16)]
        both = jnp.concatenate(halves, axis=1)
        part = jnp.dot(matrix[...], both, preferred_element_type=F32).astype(BF)
        for half in range(2):
            one = part[:, half * COLS : (half + 1) * COLS].reshape(2 * NB, 16, COLS)
            out[2 * half, :, c] = one[:, :QUARTER]
            out[2 * half + 1, :, c] = one[:, QUARTER:]


BONDS = (2 * NB, 3, QUARTER, COLS)


def forward(terms, matrix):
    return pl.pallas_call(
        forward_body,
        out_shape=jax.ShapeDtypeStruct((4,) + BONDS, BF),
        in_specs=[VM, VM],
        out_specs=VM,
        cost_estimate=cost(2 * 256 * 1024 * 768, 3 << 20),
        compiler_params=SMALL,
        name="forward",
    )(terms, matrix)


def mix_body(parts, matrix, out):
    total = parts[0].astype(F32)
    for k in range(1, 4):
        total += parts[k].astype(F32)
    flat = total.reshape(6 * NB * QUARTER, COLS)
    high = flat.astype(BF)
    rest = flat - high.astype(F32)
    middle = rest.astype(BF)
    low = (rest - middle.astype(F32)).astype(BF)
    split = jnp.concatenate([high, middle, low], axis=1)
    mixed = jnp.dot(matrix[...], split, preferred_element_type=F32)
    mixed = mixed[:, :COLS] + (mixed[:, COLS : 2 * COLS] + mixed[:, 2 * COLS :])
    out[...] = mixed.reshape(BONDS).astype(BF)


def mix(parts, matrix):
    return pl.pallas_call(
        mix_body,
        out_shape=jax.ShapeDtypeStruct(BONDS, BF),
        in_specs=[VM] * 2,
        out_specs=VM,
        cost_estimate=cost(2 * 384 * 384 * 384, 1 << 20),
        compiler_params=SMALL,
        name="mix",
    )(parts, matrix)


def backward_body(parts, terms, matrix, out):
    scale = 1.0 / math.sqrt(NB * SOURCES)
    for c in range(3):
        row = c * ROWS
        halves = [
            jnp.concatenate([parts[2 * h, :, c], parts[2 * h + 1, :, c]], axis=1).reshape(
                2 * NB * 16, COLS
            )
            for h in range(2)
        ]
        back = jnp.dot(
            matrix[...], jnp.concatenate(halves, axis=1), preferred_element_type=F32
        )
        for half in range(2):
            here = row + half * 16
            one = back[:, half * COLS : (half + 1) * COLS].reshape(GROUP, 16, COLS)
            flow = terms[:, here : here + 16, :].astype(F32) + one * scale
            out[:, here : here + 16, :] = flow.astype(BF)


def backward(parts, terms, matrix):
    return pl.pallas_call(
        backward_body,
        out_shape=jax.ShapeDtypeStruct((GROUP, 3 * ROWS, COLS), BF),
        in_specs=[VM] * 3,
        out_specs=VM,
        cost_estimate=cost(2 * 256 * 1024 * 768, 5 << 20),
        compiler_params=SMALL,
        name="backward",
    )(parts, terms, matrix)


def finish_body(pieces, out, held, sems):
    def copy(k):
        c, r = divmod(k, 4)
        return pltpu.make_async_copy(held.at[c, r], out.at[c, r], sems.at[k])

    for k in range(12):
        c, r = divmod(k, 4)
        for w in range(OWNERS):
            held[c, r, w * ROWS : (w + 1) * ROWS, :] = pieces[w, r, c].astype(F32)
        if k > 0:
            copy(k - 1).start()
    copy(11).start()
    for k in range(12):
        copy(k).wait()


def finish(pieces):
    return pl.pallas_call(
        finish_body,
        out_shape=jax.ShapeDtypeStruct((3, 4, NI, COLS), F32),
        in_specs=[VM],
        out_specs=pl.BlockSpec(memory_space=pl.ANY),
        scratch_shapes=[pltpu.VMEM((3, 4, NI, COLS), F32), pltpu.SemaphoreType.DMA((12,))],
        cost_estimate=cost(1 << 20, 5 << 20),
        compiler_params=SMALL,
        name="finish",
    )(pieces)


def turn(value, axis, shift):
    return lax.ppermute(value, axis, [(k, (k + shift) % 4) for k in range(4)])


def local(
    vertex, formfactors, propagator, loop_mom, bond_disp, proj_channel, proj_bond, proj_phase
):
    x = lax.axis_index("x")
    z = lax.axis_index("z4")
    owner = lax.axis_index(("z4", "z2", "y", "c"))
    place_x = jnp.reshape(x, (1,)).astype(jnp.int32)

    sent = {}
    source = vertex
    for s in (2, 1, 3):
        sent[s] = lax.dynamic_index_in_dim(source, (x + s) % 4, 1, keepdims=False)
        source, sent[s] = lax.optimization_barrier((source, sent[s]))
    v2 = turn(sent[2], "x", 2)
    v1 = turn(sent[1], "x", 1)
    v3 = turn(sent[3], "x", 3)

    weights = loop_weights(propagator, loop_mom, 4 * owner + x)
    phases = phase_table(bond_disp, GROUP * z + jnp.arange(GROUP, dtype=jnp.int32))
    there = times_identity(phases, 16).astype(BF)
    back = times_identity(phases.T, 16).astype(BF)
    mixing = mixing_matrix(proj_channel, proj_bond, proj_phase)
    mixing = times_identity(mixing, QUARTER).astype(BF)


    k0, turned_form, v0 = own_rows(place_x, vertex, formfactors, weights)
    k2 = panel_rows(v2, formfactors, turned_form, weights)
    increment = last_rows(
        place_x, v0, v1, v2, v3, formfactors, turned_form, weights, k0, k2
    )
    increment = increment.reshape(GROUP, 3 * ROWS, COLS)
    terms = lax.all_to_all(increment, ("z2", "y", "c", "x"), 0, 0, tiled=True)

    sums = lax.all_to_all(forward(terms, there), "z4", 0, 0, tiled=True)
    parts = lax.all_gather(mix(sums, mixing), "z4", axis=0, tiled=False)
    flow = backward(parts, terms, back)
    flow = flow.reshape(OWNERS, 4 * 3 * ROWS, COLS)
    pieces = lax.all_to_all(flow, ("z2", "y", "c"), 0, 0, tiled=True)
    return finish(pieces.reshape(OWNERS, 4, 3, ROWS, COLS))


def solution(mesh):
    fine = Mesh(mesh.devices.reshape(4, 2, 4, 2, 4), ("z4", "z2", "y", "c", "x"))
    placed = P(None, ("z4", "z2", "y", "c"), None, "x")
    in_specs = (placed, P(), P(), P(), P(), P(), P(), P())
    return jax.shard_map(local, mesh=fine, in_specs=in_specs, out_specs=placed, check_vma=False)
```

profile of v0, /device:TPU:1, one launch (start us, length us, event | category | flops | bytes accessed | tf_op | source)
XLA Modules:
  0.0 128.9 jit_solution(3715575362207918192)
XLA Ops:
  0.0 0.0 copy-start
  0.0 0.0 copy-start.5
  0.0 1.1 dynamic-slice_bitcast_fusion.2
  1.2 1.0 dynamic-slice_bitcast_fusion.1
  2.2 0.0 copy-done
  2.2 0.8 dynamic-slice_bitcast_fusion
  3.0 3.3 %collective-permute-start.2 = (bf16[3,512,128]{2,1,0:T(8,128)(2,1)}, bf16[3,512,128]{2,1,0:T(8,128)(2,1)S(1)}, u32[]{:S(2)}, u32[]{:S(2)}) collective-permute-start(bf16[3,512,128]{2,1,0:T(8,128)(2,1)} %dynamic-slice_bitcast_fusion), channel_id=1, source_target_pairs={{0,3},{1,0},{2,1},{3,2},{4,7},{5,4},{6,5},{7,6},{8,11},{9,8},{10,9... | collective-permute-start | bytes 1179656 | tf_op jit(solution)/shard_map/ppermute | solution.py:347
  6.3 0.5 collective-permute-start.1
  6.8 0.6 collective-permute-start
  7.5 0.0 copy-done.5
  7.5 0.3 select_reduce_fusion
  7.8 1.5 %fusion = f32[4,2048]{1,0:T(4,128)S(1)} fusion(s32[2048]{0:T(1024)} %param.11, f32[3,256]{1,0:T(4,128)S(1)} %select_reduce_fusion, f32[1,256]{1,0:T(1,128)S(1)} %bitcast.29), kind=kOutput, calls=%fused_computation.1 | convolution fusion | flops 25691136 | bytes 45056 | tf_op jit(solution)/shard_map/nk,kl->nl/dot_general | solution.py:55
  9.3 0.0 copy-start.1
  9.3 1.6 %copy-done.1 = bf16[2048,512]{1,0:T(8,128)(2,1)S(1)} copy-done((bf16[2048,512]{1,0:T(8,128)(2,1)S(1)}, bf16[2048,512]{1,0:T(8,128)(2,1)}, u32[]{:S(2)}) %copy-start.1) | copy-done | bytes 2097176
  10.9 2.7 %own_rows.1 = (bf16[384,512]{1,0:T(8,128)(2,1)S(1)}, bf16[512,2048]{1,0:T(8,128)(2,1)S(1)}, bf16[3,512,128]{2,1,0:T(8,128)(2,1)S(1)}) custom-call(s32[1]{0:T(128)} %bitcast.place, bf16[3,4,512,128]{3,2,1,0:T(8,128)(2,1)S(1)} %copy-done, bf16[2048,512]{1,0:T(8,128)(2,1)S(1)} %copy-done.1, f32[3,2048]{1,0:T(4,128)S(1)} %fusion.32.weights), custom_call_target="tpu_custom_call" | custom-call | flops 1610612736 | bytes 3145728 | tf_op jit(solution)/shard_map/own_rows/pallas_call | solution.py:183
  13.6 3.9 %collective-permute-done.1.panel.v2 = bf16[3,512,128]{2,1,0:T(8,128)(2,1)S(1)} collective-permute-done((bf16[3,512,128]{2,1,0:T(8,128)(2,1)S(1)}, bf16[3,512,128]{2,1,0:T(8,128)(2,1)S(1)}, u32[]{:S(2)}, u32[]{:S(2)}) %collective-permute-start.1) | collective-permute-done | bytes 393248 | tf_op jit(solution)/shard_map/ppermute | solution.py:347
  17.5 2.0 %panel_rows.1.k2 = bf16[384,512]{1,0:T(8,128)(2,1)S(1)} custom-call(bf16[3,512,128]{2,1,0:T(8,128)(2,1)S(1)} %collective-permute-done.1.panel.v2, bf16[2048,512]{1,0:T(8,128)(2,1)S(1)} %copy-done.1, bf16[512,2048]{1,0:T(8,128)(2,1)S(1)} %get-tuple-element.19.turned_form, f32[3,2048]{1,0:T(4,128)S(1)} %fusion.32.weights), custom_call_target="tpu_custom_call" | custom-call | flops 1610612736 | bytes 3145728 | tf_op jit(solution)/shard_map/panel_rows/pallas_call | solution.py:200
  19.6 0.0 collective-permute-done.2.v3
  19.6 7.7 %collective-permute-done.v1 = bf16[3,512,128]{2,1,0:T(8,128)(2,1)S(1)} collective-permute-done((bf16[3,512,128]{2,1,0:T(8,128)(2,1)S(1)}, bf16[3,512,128]{2,1,0:T(8,128)(2,1)S(1)}, u32[]{:S(2)}, u32[]{:S(2)}) %collective-permute-start) | collective-permute-done | bytes 393248 | tf_op jit(solution)/shard_map/ppermute | solution.py:347
  27.2 5.5 %last_rows.1 = bf16[16,4,3,32,128]{4,3,2,1,0:T(8,128)(2,1)} custom-call(s32[1]{0:T(128)} %bitcast.place, bf16[3,512,128]{2,1,0:T(8,128)(2,1)S(1)} %get-tuple-element.13.v0, bf16[3,512,128]{2,1,0:T(8,128)(2,1)S(1)} %collective-permute-done.v1, bf16[3,512,128]{2,1,0:T(8,128)(2,1)S(1)} %collective-permute-done.1.panel.v2, ...), custom_call_target="tpu_custom_call" | custom-call | flops 4026531840 | bytes 8388608 | tf_op jit(solution)/shard_map/last_rows/pallas_call | solution.py:213
  32.8 0.0 copy-start.3
  32.8 0.0 copy-start.4
  32.8 0.0 copy-start.2
  32.8 0.0 copy-start.6
  32.8 7.5 %all-to-all-start = ((bf16[64,96,128]{2,1,0:T(8,128)(2,1)}), bf16[64,96,128]{2,1,0:T(8,128)(2,1)S(1)}, u32[]{:S(2)}, u32[]{:S(2)}) async-start(bf16[64,96,128]{2,1,0:T(8,128)(2,1)} %bitcast.6), calls=%async_computation | async-start | bytes 3145728 | tf_op jit(solution)/shard_map/all_to_all | solution.py:381
  40.4 0.0 copy-done.3
  40.4 0.0 copy-done.4
  40.5 0.0 copy-done.2
  40.5 0.1 fusion.31
  40.6 0.1 fusion.15
  40.7 0.0 copy-done.6
  40.7 0.1 cosine_convert_fusion
  40.8 0.8 fusion.1.matrix
  41.7 21.3 %all-to-all-done.terms = bf16[64,96,128]{2,1,0:T(8,128)(2,1)S(1)} async-done(((bf16[64,96,128]{2,1,0:T(8,128)(2,1)}), bf16[64,96,128]{2,1,0:T(8,128)(2,1)S(1)}, u32[]{:S(2)}, u32[]{:S(2)}) %all-to-all-start) | async-done | bytes 1572896 | tf_op jit(solution)/shard_map/all_to_all | solution.py:381
  63.0 1.3 %forward.1 = bf16[4,16,3,8,128]{4,3,2,1,0:T(8,128)(2,1)} custom-call(bf16[64,96,128]{2,1,0:T(8,128)(2,1)S(1)} %all-to-all-done.terms, bf16[256,1024]{1,0:T(8,128)(2,1)S(1)} %fusion.1.matrix), custom_call_target="tpu_custom_call" | custom-call | flops 402653184 | bytes 3145728 | tf_op jit(solution)/shard_map/forward/pallas_call | solution.py:247
  64.3 7.5 %all-to-all-start.1 = ((bf16[4,16,3,8,128]{4,3,2,1,0:T(8,128)(2,1)}), bf16[4,16,3,8,128]{4,3,2,1,0:T(8,128)(2,1)S(1)}, u32[]{:S(2)}, u32[]{:S(2)}) async-start(bf16[4,16,3,8,128]{4,3,2,1,0:T(8,128)(2,1)} %forward.1), calls=%async_computation.1 | async-start | bytes 786432 | tf_op jit(solution)/shard_map/all_to_all | solution.py:383
  71.8 0.1 copy.27
  71.9 0.1 copy.28
  72.0 0.1 copy.25
  72.1 0.1 copy.26
  72.2 0.5 fusion.3.matrix
  72.8 1.0 fusion.2.matrix
  73.8 7.0 %all-to-all-done.1.parts = bf16[4,16,3,8,128]{4,3,2,1,0:T(8,128)(2,1)S(1)} async-done(((bf16[4,16,3,8,128]{4,3,2,1,0:T(8,128)(2,1)}), bf16[4,16,3,8,128]{4,3,2,1,0:T(8,128)(2,1)S(1)}, u32[]{:S(2)}, u32[]{:S(2)}) %all-to-all-start.1) | async-done | bytes 393248 | tf_op jit(solution)/shard_map/all_to_all | solution.py:383
  80.8 0.4 mix.1
  81.2 14.1 %all-gather = bf16[64,3,8,128]{3,2,1,0:T(8,128)(2,1)S(1)} all-gather(bf16[16,3,8,128]{3,2,1,0:T(8,128)(2,1)S(1)} %mix.1), channel_id=2, replica_groups=mesh['z4'=4,'z2'=2,'y'=4,'c'=2,'x'=4] {'z4'}, dimensions={0}, use_global_device_ids=true | all-gather | bytes 491520 | tf_op jit(solution)/shard_map/all_gather | solution.py:384
  95.3 0.6 backward.1
  95.9 31.1 %all_to_all.15 = bf16[16,384,128]{2,1,0:T(8,128)(2,1)S(1)} all-to-all(bf16[16,384,128]{2,1,0:T(8,128)(2,1)S(1)} %bitcast.23), channel_id=1, replica_groups=mesh['z4'=4,'z2'=2,'y'=4,'c'=2,'x'=4] {'z2','y','c'}, dimensions={0} | all-to-all | bytes 3145728 | tf_op jit(solution)/shard_map/all_to_all | solution.py:387
  127.0 1.8 %finish.1 = f32[3,4,512,128]{3,2,1,0:T(8,128)} custom-call(bf16[16,4,3,32,128]{4,3,2,1,0:T(8,128)(2,1)S(1)} %bitcast.24), custom_call_target="tpu_custom_call" | custom-call | flops 1048576 | bytes 5242880 | tf_op jit(solution)/shard_map/finish/pallas_call | solution.py:334
  (23 shorter events, 0.2 us)
Async XLA Ops:
  0.0 2.2 %copy-start = (bf16[3,4,512,128]{3,2,1,0:T(8,128)(2,1)S(1)}, bf16[3,4,512,128]{3,2,1,0:T(8,128)(2,1)}, u32[]{:S(2)}) copy-start(bf16[3,4,512,128]{3,2,1,0:T(8,128)(2,1)} %vertex.1) | copy-start | bytes 4718596
  0.0 7.5 %copy-start.5 = (f32[256]{0:T(256)S(1)}, f32[256]{0:T(256)}, u32[]{:S(2)}) copy-start(f32[256]{0:T(256)} %param.10) | copy-start | bytes 3076
  3.0 16.6 %collective-permute-start.2 = (bf16[3,512,128]{2,1,0:T(8,128)(2,1)}, bf16[3,512,128]{2,1,0:T(8,128)(2,1)S(1)}, u32[]{:S(2)}, u32[]{:S(2)}) collective-permute-start(bf16[3,512,128]{2,1,0:T(8,128)(2,1)} %dynamic-slice_bitcast_fusion), channel_id=1, source_target_pairs={{0,3},{1,0},{2,1},{3,2},{4,7},{5,4},{6,5},{7,6},{8,11},{9,8},{10,9... | collective-permute-start | bytes 1179656 | tf_op jit(solution)/shard_map/ppermute | solution.py:347
  6.3 11.3 %collective-permute-start.1 = (bf16[3,512,128]{2,1,0:T(8,128)(2,1)S(1)}, bf16[3,512,128]{2,1,0:T(8,128)(2,1)S(1)}, u32[]{:S(2)}, u32[]{:S(2)}) collective-permute-start(bf16[3,512,128]{2,1,0:T(8,128)(2,1)S(1)} %dynamic-slice_bitcast_fusion.2), channel_id=1, source_target_pairs={{0,2},{1,3},{2,0},{3,1},{4,6},{5,7},{6,4},{7,5},{8,10},{9,11},{10,... | collective-permute-start | bytes 1179656 | tf_op jit(solution)/shard_map/ppermute | solution.py:347
  6.8 20.4 %collective-permute-start = (bf16[3,512,128]{2,1,0:T(8,128)(2,1)S(1)}, bf16[3,512,128]{2,1,0:T(8,128)(2,1)S(1)}, u32[]{:S(2)}, u32[]{:S(2)}) collective-permute-start(bf16[3,512,128]{2,1,0:T(8,128)(2,1)S(1)} %dynamic-slice_bitcast_fusion.1), channel_id=1, source_target_pairs={{0,1},{1,2},{2,3},{3,0},{4,5},{5,6},{6,7},{7,4},{8,9},{9,10},{10,1... | collective-permute-start | bytes 1179656 | tf_op jit(solution)/shard_map/ppermute | solution.py:347
  9.3 1.6 %copy-start.1 = (bf16[2048,512]{1,0:T(8,128)(2,1)S(1)}, bf16[2048,512]{1,0:T(8,128)(2,1)}, u32[]{:S(2)}) copy-start(bf16[2048,512]{1,0:T(8,128)(2,1)} %form.5) | copy-start | bytes 6291460
  32.8 7.7 %copy-start.3 = (s32[3,8,4]{1,2,0:T(4,128)S(1)}, s32[3,8,4]{1,2,0:T(4,128)}, u32[]{:S(2)}) copy-start(s32[3,8,4]{1,2,0:T(4,128)} %param.15) | copy-start | bytes 1156
  32.8 7.7 %copy-start.4 = (s32[3,8,4]{1,2,0:T(4,128)S(1)}, s32[3,8,4]{1,2,0:T(4,128)}, u32[]{:S(2)}) copy-start(s32[3,8,4]{1,2,0:T(4,128)} %param.13) | copy-start | bytes 1156
  32.8 7.7 %copy-start.2 = (s32[3,8,4]{1,2,0:T(4,128)S(1)}, s32[3,8,4]{1,2,0:T(4,128)}, u32[]{:S(2)}) copy-start(s32[3,8,4]{1,2,0:T(4,128)} %param.14) | copy-start | bytes 1156
  32.8 7.9 %copy-start.6 = (s32[8,2]{0,1:T(2,128)S(1)}, s32[8,2]{0,1:T(2,128)}, u32[]{:S(2)}) copy-start(s32[8,2]{0,1:T(2,128)} %param.12) | copy-start | bytes 196
  32.8 30.2 %all-to-all-start = ((bf16[64,96,128]{2,1,0:T(8,128)(2,1)}), bf16[64,96,128]{2,1,0:T(8,128)(2,1)S(1)}, u32[]{:S(2)}, u32[]{:S(2)}) async-start(bf16[64,96,128]{2,1,0:T(8,128)(2,1)} %bitcast.6), calls=%async_computation | async-start | bytes 3145728 | tf_op jit(solution)/shard_map/all_to_all | solution.py:381
  64.3 16.5 %all-to-all-start.1 = ((bf16[4,16,3,8,128]{4,3,2,1,0:T(8,128)(2,1)}), bf16[4,16,3,8,128]{4,3,2,1,0:T(8,128)(2,1)S(1)}, u32[]{:S(2)}, u32[]{:S(2)}) async-start(bf16[4,16,3,8,128]{4,3,2,1,0:T(8,128)(2,1)} %forward.1), calls=%async_computation.1 | async-start | bytes 786432 | tf_op jit(solution)/shard_map/all_to_all | solution.py:383
where the time goes:
time: 129 us
  blocking collectives  45.2 us (35%)
  waiting for transfers between devices  40 us (31%)
  starting transfers between devices  19.4 us (15%)
  Pallas kernels  14.3 us (11%)
  local copies, waits for them, and re-layouts  4.96 us (4%)
  matrix products  3.81 us (3%)
    all_to_all x1, blocking collectives, local(): pieces = lax.all_to_all(flow, ('z2', 'y', 'c'), 0, 0, tiled=True)  31.1 us
    all_to_all x1, waiting for transfers between devices, local(): terms = lax.all_to_all(increment, ('z2', 'y', 'c', 'x'), 0, 0, tiled=True)  21.3 us
    all_gather x1, blocking collectives, local(): parts = lax.all_gather(mix(sums, mixing), 'z4', axis=0, tiled=False)  14.1 us
    ppermute x3, waiting for transfers between devices, turn(): return lax.ppermute(value, axis, [(k, (k + shift) % 4) for k in range(4)])  11.6 us
    all_to_all x1, starting transfers between devices, local(): terms = lax.all_to_all(increment, ('z2', 'y', 'c', 'x'), 0, 0, tiled=True)  7.49 us
    all_to_all x1, starting transfers between devices, local(): sums = lax.all_to_all(forward(terms, there), 'z4', 0, 0, tiled=True)  7.48 us
    all_to_all x1, waiting for transfers between devices, local(): sums = lax.all_to_all(forward(terms, there), 'z4', 0, 0, tiled=True)  7.03 us
    pallas_call x1, Pallas kernels, last_rows(): pl.pallas_call(last_body, out_shape=jax.ShapeDtypeStruct((OWNERS, 4, 3, R...  5.5 us
  transfers between devices with their start and end apart: 5, of which 4 were waited for; matrix products, arithmetic and copies ran while one was open for 4% of the time, Pallas kernels for 4%

commit v1 on v0

--- a/solution.py
+++ b/solution.py
@@ -64,21 +64,21 @@
     return jnp.concatenate([jnp.cos(angles), -jnp.sin(angles)], axis=0).astype(BF)
 
 
-def spread(count, each):
-    long = lax.broadcasted_iota(jnp.int32, (count * each, count), 0) // each
-    short = lax.broadcasted_iota(jnp.int32, (count * each, count), 1)
-    return (long == short).astype(BF)
+def hot(shape, axis, each):
+    long = lax.broadcasted_iota(jnp.int32, shape, axis) // each
+    short = lax.broadcasted_iota(jnp.int32, shape, 1 - axis)
+    return jnp.where(long == short, 1.0, 0.0).astype(BF)
 
 
 def times_identity(matrix, each):
     rows, cols = matrix.shape
-    wide = jnp.einsum("rc,kc->rk", matrix, spread(cols, each), preferred_element_type=F32)
-    full = jnp.einsum(
-        "mr,rk->mk", spread(rows, each), wide.astype(BF), preferred_element_type=F32
+    wide = jnp.dot(matrix, hot((cols, cols * each), 1, each), preferred_element_type=F32)
+    full = jnp.dot(
+        hot((rows * each, rows), 0, each), wide.astype(BF), preferred_element_type=F32
     )
     row_id = lax.broadcasted_iota(jnp.int32, full.shape, 0) % each
     col_id = lax.broadcasted_iota(jnp.int32, full.shape, 1) % each
-    return jnp.where(row_id == col_id, full, 0.0)
+    return jnp.where(row_id == col_id, full, 0.0).astype(BF)
 
 
 def mixing_matrix(proj_channel, proj_bond, proj_phase):
@@ -129,13 +129,18 @@
     out[...] = total[...].astype(BF)
 
 
-def panel_body(panel, form, turned_form, weights, out, total):
+def panel_body(
+    panel, form, turned_form, weights, phases, turned_phases, table, out, there, back, mixing, total
+):
     kernel_rows([lambda c: panel[c]], form, turned_form, weights, total)
     out[...] = total[...].astype(BF)
+    there[...] = times_identity(phases[...], 16)
+    back[...] = times_identity(turned_phases[...], 16)
+    mixing[...] = times_identity(table[...], QUARTER)
 
 
 def last_body(
-    place, v0, v1, v2, v3, form, turned_form, weights, k0, k2, out, total, whole, k13, held, sems
+    place, v0, v1, v2, v3, form, turned_form, weights, k0, k2, out, total, whole, k13
 ):
     x = place[0]
     kernel_rows([lambda c: v1[c], lambda c: v3[c]], form, turned_form, weights, total)
@@ -143,9 +148,6 @@
     for c in range(3):
         for s in range(4):
             whole[c, lax.rem(x + 4 - s, 4)] = (v0, v1, v2, v3)[s][c]
-
-    def copy(c):
-        return pltpu.make_async_copy(held.at[c], out.at[:, :, c], sems.at[c])
 
     for c in range(3):
         row = c * COLS
@@ -162,12 +164,7 @@
         inc = nt_dot(natural, rows).astype(BF)
         for s in range(4):
             part = inc[:, s * COLS : (s + 1) * COLS].reshape(OWNERS, 1, ROWS, COLS)
-            held[c, :, pl.ds(lax.rem(x + 4 - s, 4), 1)] = part
-        if c > 0:
-            copy(c - 1).start()
-    copy(2).start()
-    for c in range(3):
-        copy(c).wait()
+            out[:, pl.ds(lax.rem(x + 4 - s, 4), 1), c] = part
 
 
 VM = pl.BlockSpec(memory_space=pltpu.VMEM)
@@ -196,17 +193,22 @@
     )(place, vertex, form, weights)
 
 
-def panel_rows(panel, form, turned_form, weights):
+def panel_rows(panel, form, turned_form, weights, phases, turned_phases, table):
     return pl.pallas_call(
         panel_body,
-        out_shape=jax.ShapeDtypeStruct((3 * COLS, NI), BF),
-        in_specs=[VM] * 4,
-        out_specs=VM,
+        out_shape=[
+            jax.ShapeDtypeStruct((3 * COLS, NI), BF),
+            jax.ShapeDtypeStruct((2 * NB * 16, GROUP * 16), BF),
+            jax.ShapeDtypeStruct((GROUP * 16, 2 * NB * 16), BF),
+            jax.ShapeDtypeStruct((6 * NB * QUARTER, 6 * NB * QUARTER), BF),
+        ],
+        in_specs=[VM] * 7,
+        out_specs=[VM] * 4,
         scratch_shapes=[pltpu.VMEM((3 * COLS, NI), F32)],
         cost_estimate=cost(KERNEL_FLOPS, 3 << 20),
         compiler_params=SMALL,
         name="panel_rows",
-    )(panel, form, turned_form, weights)
+    )(panel, form, turned_form, weights, phases, turned_phases, table)
 
 
 def last_rows(place, v0, v1, v2, v3, form, turned_form, weights, k0, k2):
@@ -214,13 +216,11 @@
         last_body,
         out_shape=jax.ShapeDtypeStruct((OWNERS, 4, 3, ROWS, COLS), BF),
         in_specs=[SM] + [VM] * 9,
-        out_specs=HB,
+        out_specs=VM,
         scratch_shapes=[
             pltpu.VMEM((6 * COLS, NI), F32),
             pltpu.VMEM((3, 4, NI, COLS), BF),
             pltpu.VMEM((6 * COLS, NI), BF),
-            pltpu.VMEM((3, OWNERS, 4, ROWS, COLS), BF),
-            pltpu.SemaphoreType.DMA((3,)),
         ],
         cost_estimate=cost(2 * KERNEL_FLOPS + 2 * 3 * NI * NI * NI, 8 << 20),
         compiler_params=SMALL,
@@ -366,14 +366,12 @@
 
     weights = loop_weights(propagator, loop_mom, 4 * owner + x)
     phases = phase_table(bond_disp, GROUP * z + jnp.arange(GROUP, dtype=jnp.int32))
-    there = times_identity(phases, 16).astype(BF)
-    back = times_identity(phases.T, 16).astype(BF)
-    mixing = mixing_matrix(proj_channel, proj_bond, proj_phase)
-    mixing = times_identity(mixing, QUARTER).astype(BF)
-
+    table = mixing_matrix(proj_channel, proj_bond, proj_phase)
 
     k0, turned_form, v0 = own_rows(place_x, vertex, formfactors, weights)
-    k2 = panel_rows(v2, formfactors, turned_form, weights)
+    k2, there, back, mixing = panel_rows(
+        v2, formfactors, turned_form, weights, phases, phases.T, table
+    )
     increment = last_rows(
         place_x, v0, v1, v2, v3, formfactors, turned_form, weights, k0, k2
     )

time: 129 us -> 130 us (level)
  blocking collectives: 45.2 us -> 93.6 us
  waiting for transfers between devices: 40 us -> 10.2 us
  starting transfers between devices: 19.4 us -> 5.03 us
  matrix products: 3.81 us -> 0.75 us
    all_to_all x0 -> x2, blocking collectives: none -> 49 us  [the longest x1 31.6 us: local(): terms = lax.all_to_all(increment, ('z2', 'y', 'c', 'x'), 0, 0, tiled=True)]
    all_to_all x2 -> x0, waiting for transfers between devices: 28.4 us -> none  [the longest x1 21.3 us: local(): terms = lax.all_to_all(increment, ('z2', 'y', 'c', 'x'), 0, 0, tiled=True)]
    all_to_all x2 -> x0, starting transfers between devices: 15 us -> none  [the longest x1 7.49 us: local(): terms = lax.all_to_all(increment, ('z2', 'y', 'c', 'x'), 0, 0, tiled=True)]
    dot_general x3 -> x0, matrix products: 2.36 us -> none  [times_identity(): jnp.einsum('mr,rk->mk', spread(rows, each), wide.astype(BF), preferred_el...]
    all_gather x1, blocking collectives: 14.1 us -> 12 us  [local(): parts = lax.all_gather(mix(sums, mixing), 'z4', axis=0, tiled=False)]
    all_to_all x1, blocking collectives: 31.1 us -> 32.6 us  [local(): pieces = lax.all_to_all(flow, ('z2', 'y', 'c'), 0, 0, tiled=True)]
    ppermute x3, waiting for transfers between devices: 11.6 us -> 10.2 us  [turn(): return lax.ppermute(value, axis, [(k, (k + shift) % 4) for k in range(4)])]
  transfers between devices with their start and end apart: 5 -> 3, of which waited for: 4 -> 1; matrix products, arithmetic and copies ran while one was open for 4% -> 2% of each run, Pallas kernels for 4% -> 4%
where the time goes in v1:
time: 130 us
  blocking collectives  93.6 us (72%)
  Pallas kernels  13.1 us (10%)
  waiting for transfers between devices  10.2 us (8%)
  local copies, waits for them, and re-layouts  5.8 us (4%)
  starting transfers between devices  5.03 us (4%)
    all_to_all x1, blocking collectives, local(): pieces = lax.all_to_all(flow, ('z2', 'y', 'c'), 0, 0, tiled=True)  32.6 us
    all_to_all x1, blocking collectives, local(): terms = lax.all_to_all(increment, ('z2', 'y', 'c', 'x'), 0, 0, tiled=True)  31.6 us
    all_to_all x1, blocking collectives, local(): sums = lax.all_to_all(forward(terms, there), 'z4', 0, 0, tiled=True)  17.4 us
    all_gather x1, blocking collectives, local(): parts = lax.all_gather(mix(sums, mixing), 'z4', axis=0, tiled=False)  12 us
    ppermute x3, waiting for transfers between devices, turn(): return lax.ppermute(value, axis, [(k, (k + shift) % 4) for k in range(4)])  10.2 us
    ppermute x3, starting transfers between devices, turn(): return lax.ppermute(value, axis, [(k, (k + shift) % 4) for k in range(4)])  5.03 us
    pallas_call x1, Pallas kernels, last_rows(): pl.pallas_call(last_body, out_shape=jax.ShapeDtypeStruct((OWNERS, 4, 3, R...  4.48 us
    squeeze x3, local copies, waits for them, and re-layouts, local(): sent[s] = lax.dynamic_index_in_dim(source, (x + s) % 4, 1, keepdims=False)  3.68 us
  transfers between devices with their start and end apart: 3, of which 1 were waited for; matrix products, arithmetic and copies ran while one was open for 2% of the time, Pallas kernels for 4%

profile of v1, /device:TPU:1, one launch (start us, length us, event | category | flops | bytes accessed | tf_op | source)
XLA Modules:
  0.0 129.6 jit_solution(489892098421314315)
XLA Ops:
  0.0 0.0 copy-start
  0.0 0.0 copy-start.6
  0.0 0.0 copy-start.3
  0.0 0.0 copy-start.4
  0.0 0.0 copy-start.5
  0.0 0.0 copy-start.7
  0.1 0.0 copy-start.2
  0.1 1.9 %dynamic-slice_bitcast_fusion.2 = bf16[3,512,128]{2,1,0:T(8,128)(2,1)} fusion(bf16[3,4,512,128]{3,2,1,0:T(8,128)(2,1)} %vertex.1, s32[]{:T(128)S(6)} %select_n.201), kind=kLoop, calls=%fused_computation.7 | loop fusion | bytes 786436 | tf_op jit(solution)/shard_map/jit(dynamic_index_in_dim)/squeeze | solution.py:361
  2.0 1.0 dynamic-slice_bitcast_fusion.1
  3.0 0.0 copy-done
  3.0 0.8 dynamic-slice_bitcast_fusion
  3.8 3.3 %collective-permute-start.2 = (bf16[3,512,128]{2,1,0:T(8,128)(2,1)}, bf16[3,512,128]{2,1,0:T(8,128)(2,1)S(1)}, u32[]{:S(2)}, u32[]{:S(2)}) collective-permute-start(bf16[3,512,128]{2,1,0:T(8,128)(2,1)} %dynamic-slice_bitcast_fusion), channel_id=1, source_target_pairs={{0,3},{1,0},{2,1},{3,2},{4,7},{5,4},{6,5},{7,6},{8,11},{9,8},{10,9... | collective-permute-start | bytes 1179656 | tf_op jit(solution)/shard_map/ppermute | solution.py:347
  7.1 0.0 collective-permute-start
  7.1 1.7 %collective-permute-start.1 = (bf16[3,512,128]{2,1,0:T(8,128)(2,1)}, bf16[3,512,128]{2,1,0:T(8,128)(2,1)S(1)}, u32[]{:S(2)}, u32[]{:S(2)}) collective-permute-start(bf16[3,512,128]{2,1,0:T(8,128)(2,1)} %dynamic-slice_bitcast_fusion.2), channel_id=1, source_target_pairs={{0,2},{1,3},{2,0},{3,1},{4,6},{5,7},{6,4},{7,5},{8,10},{9,11},{10,... | collective-permute-start | bytes 1179656 | tf_op jit(solution)/shard_map/ppermute | solution.py:347
  8.9 0.0 copy-done.6
  8.9 0.0 copy-done.3
  8.9 0.1 cosine_convert_fusion
  9.1 0.1 copy.28
  9.2 0.0 copy-done.4
  9.2 0.0 copy-done.5
  9.2 0.3 select_reduce_fusion
  9.5 0.0 copy-done.7
  9.5 0.8 fusion
  10.3 0.0 copy-done.2
  10.3 0.1 fusion.4
  10.4 0.1 fusion.3
  10.6 0.1 copy.31
  10.7 0.1 copy.32
  10.8 0.1 copy.29
  10.9 0.1 copy.30
  11.0 0.1 fusion.6.table
  11.1 0.0 copy-start.1
  11.1 1.6 %copy-done.1 = bf16[2048,512]{1,0:T(8,128)(2,1)S(1)} copy-done((bf16[2048,512]{1,0:T(8,128)(2,1)S(1)}, bf16[2048,512]{1,0:T(8,128)(2,1)}, u32[]{:S(2)}) %copy-start.1) | copy-done | bytes 2097176
  12.7 2.7 %own_rows.1 = (bf16[384,512]{1,0:T(8,128)(2,1)S(1)}, bf16[512,2048]{1,0:T(8,128)(2,1)S(1)}, bf16[3,512,128]{2,1,0:T(8,128)(2,1)S(1)}) custom-call(s32[1]{0:T(128)} %bitcast.place, bf16[3,4,512,128]{3,2,1,0:T(8,128)(2,1)S(1)} %copy-done, bf16[2048,512]{1,0:T(8,128)(2,1)S(1)} %copy-done.1, f32[3,2048]{1,0:T(4,128)S(1)} %fusion.5.weights), custom_call_target="tpu_custom_call" | custom-call | flops 1610612736 | bytes 3145728 | tf_op jit(solution)/shard_map/own_rows/pallas_call | solution.py:180
  15.4 10.2 %collective-permute-done.1.panel.v2 = bf16[3,512,128]{2,1,0:T(8,128)(2,1)S(1)} collective-permute-done((bf16[3,512,128]{2,1,0:T(8,128)(2,1)}, bf16[3,512,128]{2,1,0:T(8,128)(2,1)S(1)}, u32[]{:S(2)}, u32[]{:S(2)}) %collective-permute-start.1) | collective-permute-done | bytes 393248 | tf_op jit(solution)/shard_map/ppermute | solution.py:347
  25.5 2.7 %panel_rows.1 = (bf16[384,512]{1,0:T(8,128)(2,1)S(1)}, bf16[256,1024]{1,0:T(8,128)(2,1)S(1)}, bf16[1024,256]{1,0:T(8,128)(2,1)S(1)}, bf16[384,384]{1,0:T(8,128)(2,1)S(1)}) custom-call(bf16[3,512,128]{2,1,0:T(8,128)(2,1)S(1)} %collective-permute-done.1.panel.v2, bf16[2048,512]{1,0:T(8,128)(2,1)S(1)} %copy-done.1, ...), custom_call_target="tpu_custom_call" | custom-call | flops 1610612736 | bytes 3145728 | tf_op jit(solution)/shard_map/panel_rows/pallas_call | solution.py:197
  28.2 0.0 collective-permute-done.2.v3
  28.2 0.0 collective-permute-done.v1
  28.2 4.5 %last_rows.1 = bf16[16,4,3,32,128]{4,3,2,1,0:T(8,128)(2,1)S(1)} custom-call(s32[1]{0:T(128)} %bitcast.place, bf16[3,512,128]{2,1,0:T(8,128)(2,1)S(1)} %get-tuple-element.17.v0, bf16[3,512,128]{2,1,0:T(8,128)(2,1)S(1)} %collective-permute-done.v1, bf16[3,512,128]{2,1,0:T(8,128)(2,1)S(1)} %collective-permute-done.1.panel.v2, ...), custom_call_target="tpu_custom_call" | custom-call | flops 4026531840 | bytes 8388608 | tf_op jit(solution)/shard_map/last_rows/pallas_call | solution.py:215
  32.7 31.6 %all_to_all.15.terms = bf16[64,96,128]{2,1,0:T(8,128)(2,1)S(1)} all-to-all(bf16[64,96,128]{2,1,0:T(8,128)(2,1)S(1)} %bitcast.26), channel_id=1, replica_groups=mesh['z4'=4,'z2'=2,'y'=4,'c'=2,'x'=4] {'z2','y','c','x'}, dimensions={0} | all-to-all | bytes 3145728 | tf_op jit(solution)/shard_map/all_to_all | solution.py:379
  64.3 0.6 forward.1
  64.9 17.4 %all_to_all.16.parts = bf16[4,16,3,8,128]{4,3,2,1,0:T(8,128)(2,1)S(1)} all-to-all(bf16[4,16,3,8,128]{4,3,2,1,0:T(8,128)(2,1)S(1)} %forward.1), channel_id=1, replica_groups=mesh['z4'=4,'z2'=2,'y'=4,'c'=2,'x'=4] {'z4'}, dimensions={0} | all-to-all | bytes 786432 | tf_op jit(solution)/shard_map/all_to_all | solution.py:381
  82.3 0.4 mix.1
  82.6 12.0 %all-gather = bf16[64,3,8,128]{3,2,1,0:T(8,128)(2,1)S(1)} all-gather(bf16[16,3,8,128]{3,2,1,0:T(8,128)(2,1)S(1)} %mix.1), channel_id=2, replica_groups=mesh['z4'=4,'z2'=2,'y'=4,'c'=2,'x'=4] {'z4'}, dimensions={0}, use_global_device_ids=true | all-gather | bytes 491520 | tf_op jit(solution)/shard_map/all_gather | solution.py:382
  94.7 0.6 backward.1
  95.3 32.6 %all_to_all.17 = bf16[16,384,128]{2,1,0:T(8,128)(2,1)S(1)} all-to-all(bf16[16,384,128]{2,1,0:T(8,128)(2,1)S(1)} %bitcast.24), channel_id=1, replica_groups=mesh['z4'=4,'z2'=2,'y'=4,'c'=2,'x'=4] {'z2','y','c'}, dimensions={0} | all-to-all | bytes 3145728 | tf_op jit(solution)/shard_map/all_to_all | solution.py:385
  127.8 1.8 %finish.1 = f32[3,4,512,128]{3,2,1,0:T(8,128)} custom-call(bf16[16,4,3,32,128]{4,3,2,1,0:T(8,128)(2,1)S(1)} %bitcast.25), custom_call_target="tpu_custom_call" | custom-call | flops 1048576 | bytes 5242880 | tf_op jit(solution)/shard_map/finish/pallas_call | solution.py:334
  (15 shorter events, 0.2 us)
Async XLA Ops:
  0.0 3.0 %copy-start = (bf16[3,4,512,128]{3,2,1,0:T(8,128)(2,1)S(1)}, bf16[3,4,512,128]{3,2,1,0:T(8,128)(2,1)}, u32[]{:S(2)}) copy-start(bf16[3,4,512,128]{3,2,1,0:T(8,128)(2,1)} %vertex.1) | copy-start | bytes 4718596
  0.0 8.9 %copy-start.6 = (s32[8,2]{0,1:T(2,128)S(1)}, s32[8,2]{0,1:T(2,128)}, u32[]{:S(2)}) copy-start(s32[8,2]{0,1:T(2,128)} %param.12) | copy-start | bytes 196
  0.0 8.9 %copy-start.3 = (s32[3,8,4]{1,2,0:T(4,128)S(1)}, s32[3,8,4]{1,2,0:T(4,128)}, u32[]{:S(2)}) copy-start(s32[3,8,4]{1,2,0:T(4,128)} %param.15) | copy-start | bytes 1156
  0.0 9.1 %copy-start.4 = (s32[3,8,4]{1,2,0:T(4,128)S(1)}, s32[3,8,4]{1,2,0:T(4,128)}, u32[]{:S(2)}) copy-start(s32[3,8,4]{1,2,0:T(4,128)} %param.13) | copy-start | bytes 1156
  0.0 9.2 %copy-start.5 = (f32[256]{0:T(256)S(1)}, f32[256]{0:T(256)}, u32[]{:S(2)}) copy-start(f32[256]{0:T(256)} %param.10) | copy-start | bytes 3076
  0.0 9.5 %copy-start.7 = (s32[2048]{0:T(1024)S(1)}, s32[2048]{0:T(1024)}, u32[]{:S(2)}) copy-start(s32[2048]{0:T(1024)} %param.11) | copy-start | bytes 24580
  0.1 10.3 %copy-start.2 = (s32[3,8,4]{1,2,0:T(4,128)S(1)}, s32[3,8,4]{1,2,0:T(4,128)}, u32[]{:S(2)}) copy-start(s32[3,8,4]{1,2,0:T(4,128)} %param.14) | copy-start | bytes 1156
  3.8 24.4 %collective-permute-start.2 = (bf16[3,512,128]{2,1,0:T(8,128)(2,1)}, bf16[3,512,128]{2,1,0:T(8,128)(2,1)S(1)}, u32[]{:S(2)}, u32[]{:S(2)}) collective-permute-start(bf16[3,512,128]{2,1,0:T(8,128)(2,1)} %dynamic-slice_bitcast_fusion), channel_id=1, source_target_pairs={{0,3},{1,0},{2,1},{3,2},{4,7},{5,4},{6,5},{7,6},{8,11},{9,8},{10,9... | collective-permute-start | bytes 1179656 | tf_op jit(solution)/shard_map/ppermute | solution.py:347
  7.1 21.1 %collective-permute-start = (bf16[3,512,128]{2,1,0:T(8,128)(2,1)S(1)}, bf16[3,512,128]{2,1,0:T(8,128)(2,1)S(1)}, u32[]{:S(2)}, u32[]{:S(2)}) collective-permute-start(bf16[3,512,128]{2,1,0:T(8,128)(2,1)S(1)} %dynamic-slice_bitcast_fusion.1), channel_id=1, source_target_pairs={{0,1},{1,2},{2,3},{3,0},{4,5},{5,6},{6,7},{7,4},{8,9},{9,10},{10,1... | collective-permute-start | bytes 1179656 | tf_op jit(solution)/shard_map/ppermute | solution.py:347
  7.1 18.5 %collective-permute-start.1 = (bf16[3,512,128]{2,1,0:T(8,128)(2,1)}, bf16[3,512,128]{2,1,0:T(8,128)(2,1)S(1)}, u32[]{:S(2)}, u32[]{:S(2)}) collective-permute-start(bf16[3,512,128]{2,1,0:T(8,128)(2,1)} %dynamic-slice_bitcast_fusion.2), channel_id=1, source_target_pairs={{0,2},{1,3},{2,0},{3,1},{4,6},{5,7},{6,4},{7,5},{8,10},{9,11},{10,... | collective-permute-start | bytes 1179656 | tf_op jit(solution)/shard_map/ppermute | solution.py:347
  11.1 1.6 %copy-start.1 = (bf16[2048,512]{1,0:T(8,128)(2,1)S(1)}, bf16[2048,512]{1,0:T(8,128)(2,1)}, u32[]{:S(2)}) copy-start(bf16[2048,512]{1,0:T(8,128)(2,1)} %form.5) | copy-start | bytes 6291460
